TPU v7x, 32 devices: a whole 2x2x4 slice. The times are simulated.
32 devices in a mesh: dp: 8 (over z, y), owner: 4 (over x, core).
Axes of the slice: x: 2, y: 2, z: 4, core: 2. Of those that a mesh axis runs over, the one named last changes fastest.
Arguments:
- gradients: bfloat16 [8, 4, 512, 512], P('dp', 'owner'), may hold values from -600 to 600
- block_layer: int32 [4], P('owner'), may hold values from 0 to 3
Outputs:
- update: bfloat16 [4, 512, 512], P('owner', 'dp')
All inputs are finite; a program needn't handle non-finite values.
Results may differ from a plain program's by a relative error of at most 0.0062.
Values may be sent and summed in bfloat16 or wider, within the bound.
A program may use at most 64 MiB of HBM per device.

v0:
```python
import functools

import jax
import jax.numpy as jnp
from jax import lax
from jax.experimental import pallas as pl
from jax.experimental.pallas import tpu as pltpu
from jax.sharding import PartitionSpec as P

LAYERS = 4
ITERS = 3
TILE = 128
LAG = 1
BF16 = jnp.bfloat16
F32 = jnp.float32
MESH = pl.DeviceIdType.MESH


def mm(a, b):
    return jnp.dot(a.astype(BF16), b.astype(BF16), preferred_element_type=F32)


def upper_tiles(size_b):
    t = size_b // TILE
    return [(i, j) for i in range(t) for j in range(i, t)]


def pack(gram, acc_ref, first, size_b):
    tiles = upper_tiles(size_b)
    per_piece = acc_ref.shape[1] // TILE
    for n, (i, j) in enumerate(tiles):
        block = gram[i * TILE:(i + 1) * TILE, j * TILE:(j + 1) * TILE]
        row = n % per_piece * TILE
        acc_ref[first + n // per_piece, row:row + TILE, :] = block.astype(BF16)
    for n in range(len(tiles), 2 * per_piece):
        row = n % per_piece * TILE
        acc_ref[first + n // per_piece, row:row + TILE, :] = jnp.zeros((TILE, TILE), BF16)


def unpack(gath_ref, first, stat_ref, size_b):
    per_piece = gath_ref.shape[1] // TILE
    for n, (i, j) in enumerate(upper_tiles(size_b)):
        row = n % per_piece * TILE
        block = gath_ref[first + n // per_piece, row:row + TILE, :].astype(F32)
        stat_ref[i * TILE:(i + 1) * TILE, j * TILE:(j + 1) * TILE] = block
        if i != j:
            stat_ref[j * TILE:(j + 1) * TILE, i * TILE:(i + 1) * TILE] = block.T


def inverse_root(gath_ref, first, stat_ref, root_ref, size_b):
    unpack(gath_ref, first, stat_ref, size_b)
    rows = lax.broadcasted_iota(jnp.int32, (size_b, size_b), 0)
    cols = lax.broadcasted_iota(jnp.int32, (size_b, size_b), 1)
    diag = rows == cols
    stat = stat_ref[...]
    trace = jnp.sum(jnp.where(diag, stat, 0.0), keepdims=True)
    ridge = 0.01 * trace / size_b + 1e-06
    shifted = stat + jnp.where(diag, ridge, 0.0)
    norm2 = jnp.sum(shifted * shifted, keepdims=True)
    m = shifted * lax.rsqrt(norm2)
    a, y = 1.25, -0.25 * m
    for step in range(1, ITERS):
        yield
        square = mm(m, m)
        once = (25.0 * m - 10.0 * square + mm(m, square)) * 0.0625
        yield
        m = 1.5625 * once + mm((square - 10.0 * m) * 0.0625, once)
        y = 1.25 * y - (0.25 * a) * m - 0.25 * mm(y, m)
        a = 1.25 * a
    scale = lax.rsqrt(jnp.sqrt(jnp.sqrt(norm2)))
    root_ref[...] = (scale * (y + jnp.where(diag, a, 0.0))).astype(BF16)


def label_bit(me, number):
    d = 1 << number
    mine = me // d % 2
    return mine, me + d * (1 - 2 * mine)


class Piece:
    def __init__(self, index, me, order, acc, gath, landing, send, recv, target):
        self.index, self.me, self.order = index, me, order
        self.acc, self.gath, self.landing = acc, gath, landing
        self.send, self.recv, self.target = send, recv, target
        self.start_row, self.length = 0, acc.shape[0]
        self.copy, self.offset = None, 0

    def bit(self, number):
        return label_bit(self.me, number)

    def rows(self, first, length):
        return pl.ds(pl.multiple_of(first, 16), length)

    def start(self, step):
        last = len(self.order) - 1
        mine, partner = self.bit(self.order[last - abs(last - step)])
        if step < last:
            half = self.length // 2
            src = self.acc.at[self.rows(self.start_row + (1 - mine) * half, half)]
            dst = self.landing.at[pl.ds(self.offset, half)]
        elif step == last:
            src = self.acc.at[self.rows(self.start_row, self.length)]
            dst = self.landing.at[pl.ds(self.offset, self.length)]
        else:
            here = self.rows(self.start_row, self.length)
            src, dst = self.gath.at[here], self.gath.at[here]
        self.copy = pltpu.make_async_remote_copy(
            src_ref=src,
            dst_ref=dst,
            send_sem=self.send.at[self.index, step],
            recv_sem=self.recv.at[self.index, step],
            device_id=self.target(partner),
            device_id_type=MESH,
        )
        self.copy.start()

    def finish(self, step):
        last = len(self.order) - 1
        mine, _ = self.bit(self.order[last - abs(last - step)])
        self.copy.wait()
        if step <= last:
            if step < last:
                self.length //= 2
                self.start_row = self.start_row + mine * self.length
            keep = self.rows(self.start_row, self.length)
            arrived = self.landing[pl.ds(self.offset, self.length), :].astype(F32)
            total = (self.acc[keep, :].astype(F32) + arrived).astype(BF16)
            (self.acc if step < last else self.gath)[keep, :] = total
            self.offset += self.length
        else:
            self.start_row = self.start_row - mine * self.length
            self.length *= 2


def kernel(dp_count, owners, layer_ref, g_ref, out_ref, acc_s, gath_s, land_s, acc_g, gath_g,
           land_g, stats, roots, middle, middle_rows, e_src, e_buf, send, recv, e_send, e_recv):
    me = lax.axis_index("dp")
    own = lax.axis_index("owner")
    size_b = g_ref.shape[0]
    nb = dp_count.bit_length() - 1

    barrier = pltpu.get_barrier_semaphore()
    for number in range(nb):
        _, partner = label_bit(me, number)
        pl.semaphore_signal(barrier, inc=1, device_id=(partner, own), device_id_type=MESH)
    for j in range(1, owners):
        pl.semaphore_signal(
            barrier, inc=1, device_id=(me, lax.rem(own + j, owners)), device_id_type=MESH
        )

    order_a = list(range(nb))
    order_b = order_a[1::-1] + order_a[2:]
    target = lambda partner: (partner, own)
    orders = (order_a, order_b)
    left_pieces, right_pieces = (
        [
            Piece(n, me, orders[n % 2], acc_s.at[n], gath_s.at[n], land_s.at[n], send, recv, target)
            for n in pair
        ]
        for pair in ((0, 1), (2, 3))
    )
    grad_pieces = [
        Piece(4 + n, me, orders[n], acc_g.at[n], gath_g.at[n], land_g.at[n], send, recv, target)
        for n in range(2)
    ]
    g = g_ref[...]
    width = size_b // 2
    left = lax.dot_general(g, g, (((1,), (1,)), ((), ())), preferred_element_type=F32)
    pack(left, acc_s, 0, size_b)
    pl.semaphore_wait(barrier, nb + owners - 1)
    for piece in left_pieces:
        piece.start(0)
    right = lax.dot_general(g, g, (((0,), (0,)), ((), ())), preferred_element_type=F32)
    pack(right, acc_s, 2, size_b)
    for piece in right_pieces:
        piece.start(0)
    for n in range(2):
        acc_g[n] = g[:, n * width:(n + 1) * width]

    steps = 2 * nb - 1
    left_solve = inverse_root(gath_s, 0, stats.at[0], roots.at[0], size_b)
    right_solve = inverse_root(gath_s, 2, stats.at[1], roots.at[1], size_b)

    def attend(pieces, step):
        for piece in pieces:
            piece.finish(step)
            if step + 1 < steps:
                piece.start(step + 1)

    solvers = []

    def advance():
        while solvers:
            try:
                next(solvers[0])
                return
            except StopIteration:
                solvers.pop(0)

    for turn in range(steps + LAG):
        if turn < steps:
            attend(left_pieces, turn)
            if turn + 1 == steps:
                solvers.append(left_solve)
                advance()
            attend(right_pieces, turn)
            if turn + 1 == steps:
                solvers.append(right_solve)
                advance()
        if turn == 0:
            for piece in grad_pieces:
                piece.start(0)
        if 0 <= turn - LAG < steps:
            attend(grad_pieces, turn - LAG)
            advance()
    while solvers:
        advance()

    height = out_ref.shape[0]
    mine_rows = pl.ds(pl.multiple_of(me * height, 16), height)
    halves = [slice(n * width, (n + 1) * width) for n in range(2)]
    right_root = roots[1]
    for n in range(2):
        middle[:, halves[n]] = jnp.dot(
            roots[0], gath_g[n], preferred_element_type=F32
        ).astype(BF16)
        middle_rows[:, halves[n]] = jnp.dot(
            roots[0, mine_rows, :], gath_g[n], preferred_element_type=F32
        )
    whole = jnp.dot(middle[...], right_root, preferred_element_type=F32) / dp_count
    energy = jnp.sum(whole * whole, keepdims=True)

    layer = layer_ref[0]
    sub = lax.broadcasted_iota(jnp.int32, e_src.shape, 0)
    lane = lax.broadcasted_iota(jnp.int32, e_src.shape, 1)
    mine = lane == layer
    value = jnp.where(sub == 0, energy, float(size_b * size_b))
    e_src[...] = jnp.where(mine, value, 0.0)
    copies = []
    for j in range(1, owners):
        copy = pltpu.make_async_remote_copy(
            src_ref=e_src,
            dst_ref=e_buf.at[j - 1],
            send_sem=e_send.at[j - 1],
            recv_sem=e_recv.at[j - 1],
            device_id=(me, lax.rem(own + j, owners)),
            device_id_type=MESH,
        )
        copy.start()
        copies.append(copy)
    high = middle_rows[...].astype(BF16)
    low = (middle_rows[...] - high.astype(F32)).astype(BF16)
    rows = jnp.dot(high, right_root, preferred_element_type=F32)
    rows = (rows + jnp.dot(low, right_root, preferred_element_type=F32)) / dp_count
    totals = e_src[...]
    for j, copy in enumerate(copies):
        copy.wait()
        totals += e_buf[j]
    energies = jnp.sum(jnp.where(mine & (sub == 0), totals, 0.0), keepdims=True)
    counts = jnp.sum(jnp.where(mine & (sub == 1), totals, 0.0), keepdims=True)
    out_ref[...] = (rows * lax.rsqrt(energies / counts + 1e-06)).astype(BF16)


def per_device(dp_count, owners, gradients, block_layer):
    size_b = gradients.shape[-1]
    nb = dp_count.bit_length() - 1
    used = len(upper_tiles(size_b)) * TILE
    unit = max(32 * dp_count, 2 * TILE)
    packed = -(-used // unit) * unit
    height = size_b // dp_count
    width = size_b // 2
    out = pl.pallas_call(
        functools.partial(kernel, dp_count, owners),
        out_shape=jax.ShapeDtypeStruct((height, size_b), BF16),
        in_specs=[
            pl.BlockSpec(memory_space=pltpu.SMEM),
            pl.BlockSpec(memory_space=pltpu.VMEM),
        ],
        out_specs=pl.BlockSpec(memory_space=pltpu.VMEM),
        scratch_shapes=[
            pltpu.VMEM((4, packed // 2, TILE), BF16),
            pltpu.VMEM((4, packed // 2, TILE), BF16),
            pltpu.VMEM((4, packed // 2, TILE), BF16),
            pltpu.VMEM((2, size_b, width), BF16),
            pltpu.VMEM((2, size_b, width), BF16),
            pltpu.VMEM((2, size_b, width), BF16),
            pltpu.VMEM((2, size_b, size_b), F32),
            pltpu.VMEM((2, size_b, size_b), BF16),
            pltpu.VMEM((size_b, size_b), BF16),
            pltpu.VMEM((height, size_b), F32),
            pltpu.VMEM((8, TILE), F32),
            pltpu.VMEM((owners - 1, 8, TILE), F32),
            pltpu.SemaphoreType.DMA((6, 2 * nb - 1)),
            pltpu.SemaphoreType.DMA((6, 2 * nb - 1)),
            pltpu.SemaphoreType.DMA((owners - 1,)),
            pltpu.SemaphoreType.DMA((owners - 1,)),
        ],
        compiler_params=pltpu.CompilerParams(
            collective_id=0, has_side_effects=True, vmem_limit_bytes=48 * 1024 * 1024
        ),
    )(block_layer, gradients[0, 0])
    return out[None]


def solution(mesh):
    return jax.shard_map(
        functools.partial(per_device, mesh.shape["dp"], mesh.shape["owner"]),
        mesh=mesh,
        in_specs=(P("dp", "owner", None, None), P("owner")),
        out_specs=P("owner", "dp", None),
        check_vma=False,
    )
```

profile of v0, /device:TPU:0, one launch (start us, length us, event | category | flops | bytes accessed | tf_op | source)
XLA Modules:
  0.0 46.7 jit_solution(1166262417874501117)
XLA Ops:
  0.7 0.0 copy-start
  0.7 1.0 %copy-done = bf16[1,1,512,512]{3,2,1,0:T(8,128)(2,1)S(1)} copy-done((bf16[1,1,512,512]{3,2,1,0:T(8,128)(2,1)S(1)}, bf16[1,1,512,512]{3,2,1,0:T(8,128)(2,1)}, u32[]{:S(2)}) %copy-start) | copy-done | bytes 524312
  1.7 44.3 %shard_map.28 = bf16[64,512]{1,0:T(8,128)(2,1)S(1)} custom-call(s32[1]{0:T(128)S(6)} %copy.4.layer_ref, bf16[512,512]{1,0:T(8,128)(2,1)S(1)} %bitcast.2), custom_call_target="tpu_custom_call" | custom-call | tf_op jit(solution)/shard_map/pallas_call | solution.py:272
  46.0 0.6 %copy.5 = bf16[1,64,512]{2,1,0:T(8,128)(2,1)} copy(bf16[1,64,512]{2,1,0:T(8,128)(2,1)S(1)} %bitcast.3) | data formatting | bytes 131072
Async XLA Ops:
  0.7 1.0 %copy-start = (bf16[1,1,512,512]{3,2,1,0:T(8,128)(2,1)S(1)}, bf16[1,1,512,512]{3,2,1,0:T(8,128)(2,1)}, u32[]{:S(2)}) copy-start(bf16[1,1,512,512]{3,2,1,0:T(8,128)(2,1)} %param.2) | copy-start | bytes 1572868
where the time goes:
time: 46.8 us; the launch traced here: 46.7 us
  Pallas kernels  44.3 us (95%)
  local copies, waits for them, and re-layouts  1.67 us (4%)
  between operations  0.67 us (1%)
    pallas_call x1, Pallas kernels, per_device(): pl.pallas_call(functools.partial(kernel, dp_count, owners), out_shape=jax...  44.3 us
    unnamed x3, local copies, waits for them, and re-layouts  1.67 us

commit v1 on v0

v1 whole, which is shorter than its diff:
```python
import functools

import jax
import jax.numpy as jnp
from jax import lax
from jax.experimental import pallas as pl
from jax.experimental.pallas import tpu as pltpu
from jax.sharding import PartitionSpec as P

ITERS = 3
TILE = 128
EXTRA = 16
GRAD_ORDERS = (None, None)
PROGRAM = (
    "+L gR +R "
    "L +0 R +1 Lx Rx 0 1 L l l l 0x l 1x R r r r r 0 1"
)
BF16 = jnp.bfloat16
F32 = jnp.float32
MESH = pl.DeviceIdType.MESH


def mm(a, b):
    return jnp.dot(a.astype(BF16), b.astype(BF16), preferred_element_type=F32)


def iotas(rows, cols):
    return (
        lax.broadcasted_iota(jnp.int32, (rows, cols), 0),
        lax.broadcasted_iota(jnp.int32, (rows, cols), 1),
    )


def off_tiles(size_b):
    t = size_b // TILE
    return [(i, j) for i in range(t) for j in range(i + 1, t)]


def tile(array, i, j):
    return array[i * TILE:(i + 1) * TILE, j * TILE:(j + 1) * TILE]


def place(n, per_quarter):
    row = n % per_quarter * TILE
    return n // per_quarter, slice(row, row + TILE)


def pack(gram, acc_ref, size_b):
    t = size_b // TILE
    per_quarter = t * t // 8
    row, col = iotas(TILE, TILE)
    sub, _ = iotas(EXTRA, TILE)
    extra = jnp.zeros((EXTRA, TILE), F32)
    n = 0
    for d in range(0, t, 2):
        second = tile(gram, d + 1, d + 1)
        q, rows = place(n, per_quarter)
        acc_ref[q, rows, :] = jnp.where(row <= col, tile(gram, d, d), second).astype(BF16)
        diagonal = jnp.sum(jnp.where(row == col, second, 0.0), axis=0, keepdims=True)
        extra = jnp.where(sub == d // 2, diagonal, extra)
        n += 1
    for i, j in off_tiles(size_b):
        q, rows = place(n, per_quarter)
        acc_ref[q, rows, :] = tile(gram, i, j).astype(BF16)
        n += 1
    for q in range(4):
        value = extra if q == 0 else jnp.zeros((EXTRA, TILE), F32)
        acc_ref[q, per_quarter * TILE:, :] = value.astype(BF16)


def unpack(gath_ref, stat_ref, size_b):
    t = size_b // TILE
    per_quarter = t * t // 8
    row, col = iotas(TILE, TILE)
    extra = gath_ref[0, per_quarter * TILE:, :].astype(F32)
    n = 0
    for d in range(0, t, 2):
        q, rows = place(n, per_quarter)
        both = gath_ref[q, rows, :].astype(F32)
        turned = both.T
        first = jnp.where(row <= col, both, turned)
        second = jnp.where(row > col, both, turned)
        second = jnp.where(row == col, extra[d // 2:d // 2 + 1, :], second)
        for k, block in ((d, first), (d + 1, second)):
            stat_ref[k * TILE:(k + 1) * TILE, k * TILE:(k + 1) * TILE] = block
        n += 1
    for i, j in off_tiles(size_b):
        q, rows = place(n, per_quarter)
        block = gath_ref[q, rows, :].astype(F32)
        stat_ref[i * TILE:(i + 1) * TILE, j * TILE:(j + 1) * TILE] = block
        stat_ref[j * TILE:(j + 1) * TILE, i * TILE:(i + 1) * TILE] = block.T
        n += 1


def solver(gath_ref, stat_ref, size_b, result):
    unpack(gath_ref, stat_ref, size_b)
    row, col = iotas(size_b, size_b)
    diag = row == col
    stat = stat_ref[...]
    trace = jnp.sum(jnp.where(diag, stat, 0.0), keepdims=True)
    ridge = 0.01 * trace / size_b + 1e-06
    shifted = stat + jnp.where(diag, ridge, 0.0)
    norm2 = jnp.sum(shifted * shifted, keepdims=True)
    m = shifted * lax.rsqrt(norm2)
    a, y = 1.25, -0.25 * m
    for step in range(1, ITERS):
        yield
        square = mm(m, m)
        once = (25.0 * m - 10.0 * square + mm(m, square)) * 0.0625
        yield
        m = 1.5625 * once + mm((square - 10.0 * m) * 0.0625, once)
        if step + 1 < ITERS:
            y = 1.25 * y - (0.25 * a) * m - 0.25 * mm(y, m)
            a = 1.25 * a
    result["scale"] = lax.rsqrt(jnp.sqrt(jnp.sqrt(norm2)))
    result["a"], result["y"], result["m"] = a, y, m


class Piece:
    def __init__(self, me, nb, order, src, land, forward, xsend, xland, gath, send, recv, target):
        self.me, self.nb, self.order = me, nb, order
        self.src, self.land, self.forward = src, land, forward
        self.xsend, self.xland, self.gath = xsend, xland, gath
        self.send, self.recv, self.target = send, recv, target
        self.mine = lax.rem(me, 4)
        self.flow = self.run()
        self.started = []

    def partner(self, mask):
        other = self.me
        for number in range(self.nb):
            if mask >> number & 1:
                other = other + (1 - 2 * (self.me // (1 << number) % 2)) * (1 << number)
        return other

    def copy(self, src, dst, slot, mask):
        copy = pltpu.make_async_remote_copy(
            src_ref=src,
            dst_ref=dst,
            send_sem=self.send.at[slot],
            recv_sem=self.recv.at[slot],
            device_id=self.target(self.partner(mask)),
            device_id_type=MESH,
        )
        copy.start()
        self.started.append(copy)
        return copy

    def run(self):
        low = lambda mask: lax.rem(self.partner(mask), 4)
        if self.order is None:
            copies = [
                self.copy(self.src(low(mask)), self.land.at[mask - 1], mask - 1, mask)
                for mask in (1, 2, 3)
            ]
            yield
            total = self.src(self.mine)[...].astype(F32)
            for n, copy in enumerate(copies):
                copy.wait_recv()
                total += self.land[n].astype(F32)
        else:
            first, second = (1 << bit for bit in self.order)
            onward = self.copy(self.src(low(3)), self.land.at[0], 0, first)
            stay = self.copy(self.src(low(first)), self.land.at[1], 1, first)
            yield
            onward.wait_recv()
            passing = self.src(low(second))[...].astype(F32) + self.land[0].astype(F32)
            self.forward[...] = passing.astype(BF16)
            last = self.copy(self.forward, self.land.at[2], 2, second)
            yield
            stay.wait_recv()
            total = self.src(self.mine)[...].astype(F32) + self.land[1].astype(F32)
            last.wait_recv()
            total += self.land[2].astype(F32)
        for n in range(self.nb - 2):
            self.xsend[n] = total.astype(BF16)
            copy = self.copy(self.xsend.at[n], self.xland.at[n], 6 + n, 4 << n)
            yield
            copy.wait_recv()
            total = self.xsend[n].astype(F32) + self.xland[n].astype(F32)
        self.gath(self.mine)[...] = total.astype(BF16)
        own = self.gath(self.mine)
        if self.order is None:
            copies = [self.copy(own, own, 2 + mask, mask) for mask in (1, 2, 3)]
            yield
            for copy in copies:
                copy.wait_recv()
        else:
            near = self.copy(own, own, 3, second)
            far = self.copy(own, own, 4, first)
            yield
            near.wait_recv()
            other = self.gath(low(second))
            rest = self.copy(other, other, 5, first)
            yield
            far.wait_recv()
            rest.wait_recv()

    def attend(self):
        next(self.flow, None)


def kernel(dp_count, owners, layer_ref, g_ref, out_ref, acc_s, gath_s, land_s, xsend_s,
           xland_s, gath_g, land_g, forward_g, xsend_g, xland_g, stats, whole_ref, e_src, e_buf,
           send, recv, e_send, e_recv):
    me = lax.axis_index("dp")
    own = lax.axis_index("owner")
    size_b = g_ref.shape[0]
    nb = dp_count.bit_length() - 1
    quarter = size_b // 4
    chunks = len(GRAD_ORDERS)
    width = size_b // chunks

    target = lambda partner: (partner, own)
    pieces = {}
    for n, name in enumerate("LR"):
        pieces[name] = Piece(
            me, nb, None, lambda q, n=n: acc_s.at[n, q], land_s.at[n], None, xsend_s.at[n],
            xland_s.at[n], lambda q, n=n: gath_s.at[n, q], send.at[n], recv.at[n], target,
        )
    for n, order in enumerate(GRAD_ORDERS):
        def block(ref, n=n):
            def at(q):
                rows = pl.ds(pl.multiple_of(q * quarter, quarter), quarter)
                return ref.at[rows, n * width:(n + 1) * width]
            return at
        pieces[str(n)] = Piece(
            me, nb, order, block(g_ref), land_g.at[n], forward_g.at[n], xsend_g.at[n],
            xland_g.at[n], block(gath_g), send.at[2 + n], recv.at[2 + n], target,
        )

    barrier = pltpu.get_barrier_semaphore()
    masks = [1, 2, 3] + [4 << n for n in range(nb - 2)]
    for mask in masks:
        peer = pieces["L"].partner(mask)
        pl.semaphore_signal(barrier, inc=1, device_id=(peer, own), device_id_type=MESH)
    for j in range(1, owners):
        pl.semaphore_signal(
            barrier, inc=1, device_id=(me, lax.rem(own + j, owners)), device_id_type=MESH
        )
    g = g_ref[...]
    pack(
        lax.dot_general(g, g, (((1,), (1,)), ((), ())), preferred_element_type=F32),
        acc_s.at[0], size_b,
    )
    pl.semaphore_wait(barrier, len(masks) + owners - 1)

    left, right = {}, {}
    solves = {
        "l": solver(gath_s.at[0], stats.at[0], size_b, left),
        "r": solver(gath_s.at[1], stats.at[1], size_b, right),
    }
    for token in PROGRAM.split():
        if token == "gR":
            pack(
                lax.dot_general(g, g, (((0,), (0,)), ((), ())), preferred_element_type=F32),
                acc_s.at[1], size_b,
            )
        elif token in solves:
            next(solves[token], None)
        elif token[-1] == "x":
            for _ in range(nb - 2):
                pieces[token[0]].attend()
        else:
            pieces[token[-1]].attend()
    for solve in solves.values():
        for _ in solve:
            pass

    grad = gath_g[...]
    y, m, a = left["y"], left["m"], left["a"]
    y = 1.25 * y - (0.25 * a) * m - 0.25 * mm(y, m)
    middle = left["scale"] * ((1.25 * a) * grad.astype(F32) + mm(y, grad))
    half = right["a"] * middle + mm(middle, right["y"])
    whole = (right["scale"] / dp_count) * (1.25 * half - 0.25 * mm(half, right["m"]))
    whole_ref[...] = whole
    energy = jnp.sum(whole * whole, keepdims=True)

    layer = layer_ref[0]
    sub, lane = iotas(*e_src.shape)
    mine = lane == layer
    value = jnp.where(sub == 0, energy, float(size_b * size_b))
    e_src[...] = jnp.where(mine, value, 0.0)
    copies = []
    for j in range(1, owners):
        copy = pltpu.make_async_remote_copy(
            src_ref=e_src,
            dst_ref=e_buf.at[j - 1],
            send_sem=e_send.at[j - 1],
            recv_sem=e_recv.at[j - 1],
            device_id=(me, lax.rem(own + j, owners)),
            device_id_type=MESH,
        )
        copy.start()
        copies.append(copy)
    for piece in pieces.values():
        for copy in piece.started:
            copy.wait_send()
    height = out_ref.shape[0]
    rows = whole_ref[pl.ds(pl.multiple_of(me * height, 16), height), :]
    totals = e_src[...]
    for j, copy in enumerate(copies):
        copy.wait()
        totals += e_buf[j]
    energies = jnp.sum(jnp.where(mine & (sub == 0), totals, 0.0), keepdims=True)
    counts = jnp.sum(jnp.where(mine & (sub == 1), totals, 0.0), keepdims=True)
    out_ref[...] = (rows * lax.rsqrt(energies / counts + 1e-06)).astype(BF16)


def per_device(dp_count, owners, gradients, block_layer):
    size_b = gradients.shape[-1]
    nb = dp_count.bit_length() - 1
    height = size_b // dp_count
    per_quarter = (size_b // TILE) ** 2 // 8 * TILE + EXTRA
    chunks = len(GRAD_ORDERS)
    part = (size_b // 4, size_b // chunks)
    out = pl.pallas_call(
        functools.partial(kernel, dp_count, owners),
        out_shape=jax.ShapeDtypeStruct((height, size_b), BF16),
        in_specs=[
            pl.BlockSpec(memory_space=pltpu.SMEM),
            pl.BlockSpec(memory_space=pltpu.VMEM),
        ],
        out_specs=pl.BlockSpec(memory_space=pltpu.VMEM),
        scratch_shapes=[
            pltpu.VMEM((2, 4, per_quarter, TILE), BF16),
            pltpu.VMEM((2, 4, per_quarter, TILE), BF16),
            pltpu.VMEM((2, 3, per_quarter, TILE), BF16),
            pltpu.VMEM((2, nb - 2, per_quarter, TILE), BF16),
            pltpu.VMEM((2, nb - 2, per_quarter, TILE), BF16),
            pltpu.VMEM((size_b, size_b), BF16),
            pltpu.VMEM((chunks, 3, *part), BF16),
            pltpu.VMEM((chunks, *part), BF16),
            pltpu.VMEM((chunks, nb - 2, *part), BF16),
            pltpu.VMEM((chunks, nb - 2, *part), BF16),
            pltpu.VMEM((2, size_b, size_b), F32),
            pltpu.VMEM((size_b, size_b), F32),
            pltpu.VMEM((8, TILE), F32),
            pltpu.VMEM((owners - 1, 8, TILE), F32),
            pltpu.SemaphoreType.DMA((2 + chunks, 4 + nb)),
            pltpu.SemaphoreType.DMA((2 + chunks, 4 + nb)),
            pltpu.SemaphoreType.DMA((owners - 1,)),
            pltpu.SemaphoreType.DMA((owners - 1,)),
        ],
        compiler_params=pltpu.CompilerParams(
            collective_id=0, has_side_effects=True, vmem_limit_bytes=48 * 1024 * 1024
        ),
    )(block_layer, gradients[0, 0])
    return out[None]


def solution(mesh):
    return jax.shard_map(
        functools.partial(per_device, mesh.shape["dp"], mesh.shape["owner"]),
        mesh=mesh,
        in_specs=(P("dp", "owner", None, None), P("owner")),
        out_specs=P("owner", "dp", None),
        check_vma=False,
    )
```

time: 46.8 us -> 44.7 us (0.955)
  Pallas kernels: 44.3 us -> 42.2 us
    pallas_call x1, Pallas kernels: 44.3 us -> 42.2 us  [per_device(): pl.pallas_call(functools.partial(kernel, dp_count, owners), out_shape=jax...]
where the time goes in v1:
time: 44.7 us; the launch traced here: 44.5 us
  Pallas kernels  42.2 us (94%)
  local copies, waits for them, and re-layouts  1.67 us (4%)
  between operations  0.67 us (1%)
    pallas_call x1, Pallas kernels, per_device(): pl.pallas_call(functools.partial(kernel, dp_count, owners), out_shape=jax...  42.2 us
    unnamed x3, local copies, waits for them, and re-layouts  1.67 us

profile of v1, /device:TPU:0, one launch (start us, length us, event | category | flops | bytes accessed | tf_op | source)
XLA Modules:
  0.0 44.5 jit_solution(3790214352775423505)
XLA Ops:
  0.7 0.0 copy-start
  0.7 1.0 %copy-done = bf16[1,1,512,512]{3,2,1,0:T(8,128)(2,1)S(1)} copy-done((bf16[1,1,512,512]{3,2,1,0:T(8,128)(2,1)S(1)}, bf16[1,1,512,512]{3,2,1,0:T(8,128)(2,1)}, u32[]{:S(2)}) %copy-start) | copy-done | bytes 524312
  1.7 42.2 %shard_map.28 = bf16[64,512]{1,0:T(8,128)(2,1)S(1)} custom-call(s32[1]{0:T(128)S(6)} %copy.4.layer_ref, bf16[512,512]{1,0:T(8,128)(2,1)S(1)} %bitcast.2), custom_call_target="tpu_custom_call" | custom-call | tf_op jit(solution)/shard_map/pallas_call | solution.py:317
  43.9 0.6 %copy.5 = bf16[1,64,512]{2,1,0:T(8,128)(2,1)} copy(bf16[1,64,512]{2,1,0:T(8,128)(2,1)S(1)} %bitcast.3) | data formatting | bytes 131072
Async XLA Ops:
  0.7 1.0 %copy-start = (bf16[1,1,512,512]{3,2,1,0:T(8,128)(2,1)S(1)}, bf16[1,1,512,512]{3,2,1,0:T(8,128)(2,1)}, u32[]{:S(2)}) copy-start(bf16[1,1,512,512]{3,2,1,0:T(8,128)(2,1)} %param.2) | copy-start | bytes 1572868

commit v2 on v1

v2 whole, which is shorter than its diff:
```python
import functools

import jax
import jax.numpy as jnp
from jax import lax
from jax.experimental import pallas as pl
from jax.experimental.pallas import tpu as pltpu
from jax.sharding import PartitionSpec as P

ITERS = 3
TILE = 128
EXTRA = 16
LEFT_ORDERS = ((0, 1), (1, 0))
RIGHT_ORDERS = ((0, 1), (1, 0))
GRAD_ORDERS = ((0, 1), (1, 0))
PROGRAM = "BAgDAB1CDAB0DCA0B1CBA1DC0ABllDlC1ll0MDCrrrrr"
BF16 = jnp.bfloat16
F32 = jnp.float32
MESH = pl.DeviceIdType.MESH


def mm(a, b):
    return jnp.dot(a.astype(BF16), b.astype(BF16), preferred_element_type=F32)


def iotas(rows, cols):
    return (
        lax.broadcasted_iota(jnp.int32, (rows, cols), 0),
        lax.broadcasted_iota(jnp.int32, (rows, cols), 1),
    )


def off_tiles(size_b):
    t = size_b // TILE
    return [(i, j) for i in range(t) for j in range(i + 1, t)]


def tile(array, i, j):
    return array[i * TILE:(i + 1) * TILE, j * TILE:(j + 1) * TILE]


def places(size_b, pieces):
    per_quarter = (size_b // TILE) ** 2 // 8 // pieces
    for p in range(pieces):
        for q in range(4):
            for k in range(per_quarter):
                yield p, q, slice(k * TILE, (k + 1) * TILE)


def quarter_rows(size_b, pieces):
    return size_b * size_b // (8 * pieces * TILE)


def pack(gram, acc_ref, size_b, pieces):
    t = size_b // TILE
    spots = places(size_b, pieces)
    row, col = iotas(TILE, TILE)
    sub, _ = iotas(EXTRA, TILE)
    extra = jnp.zeros((EXTRA, TILE), F32)
    for d in range(0, t, 2):
        second = tile(gram, d + 1, d + 1)
        acc_ref[next(spots)] = jnp.where(row <= col, tile(gram, d, d), second).astype(BF16)
        diagonal = jnp.sum(jnp.where(row == col, second, 0.0), axis=0, keepdims=True)
        extra = jnp.where(sub == d // 2, diagonal, extra)
    for (i, j), spot in zip(off_tiles(size_b), spots):
        acc_ref[spot] = tile(gram, i, j).astype(BF16)
    for q in range(4):
        value = extra if q == 0 else jnp.zeros((EXTRA, TILE), F32)
        acc_ref[0, q, quarter_rows(size_b, pieces):, :] = value.astype(BF16)


def unpack(gath_ref, stat_ref, size_b, pieces):
    t = size_b // TILE
    spots = places(size_b, pieces)
    row, col = iotas(TILE, TILE)
    extra = gath_ref[0, 0, quarter_rows(size_b, pieces):, :].astype(F32)
    for d in range(0, t, 2):
        both = gath_ref[next(spots)].astype(F32)
        turned = both.T
        first = jnp.where(row <= col, both, turned)
        second = jnp.where(row > col, both, turned)
        second = jnp.where(row == col, extra[d // 2:d // 2 + 1, :], second)
        for k, block in ((d, first), (d + 1, second)):
            stat_ref[k * TILE:(k + 1) * TILE, k * TILE:(k + 1) * TILE] = block
    for (i, j), spot in zip(off_tiles(size_b), spots):
        block = gath_ref[spot].astype(F32)
        stat_ref[i * TILE:(i + 1) * TILE, j * TILE:(j + 1) * TILE] = block
        stat_ref[j * TILE:(j + 1) * TILE, i * TILE:(i + 1) * TILE] = block.T


def solver(gath_ref, stat_ref, size_b, pieces, result):
    unpack(gath_ref, stat_ref, size_b, pieces)
    row, col = iotas(size_b, size_b)
    diag = row == col
    stat = stat_ref[...]
    trace = jnp.sum(jnp.where(diag, stat, 0.0), keepdims=True)
    ridge = 0.01 * trace / size_b + 1e-06
    shifted = stat + jnp.where(diag, ridge, 0.0)
    norm2 = jnp.sum(shifted * shifted, keepdims=True)
    m = shifted * lax.rsqrt(norm2)
    yield
    t = (mm(m, m) - 10.0 * m) * 0.0625
    once = 1.5625 * m + mm(m, t)
    yield
    nxt = 1.5625 * once + mm(t, once)
    a = 1.5625
    y = 0.0625 * mm(once, once) - 0.3125 * (m + nxt)
    for step in range(2, ITERS):
        m = nxt
        yield
        t = (mm(m, m) - 10.0 * m) * 0.0625
        yield
        once = 1.5625 * m + mm(m, t)
        part = 1.5625 * y + a * t + mm(y, t)
        if step + 1 < ITERS:
            nxt = 1.5625 * once + mm(t, once)
        y = 1.25 * y - 0.25 * (1.5625 * a * once + mm(part, once))
        a = 1.25 * a
    result["scale"] = lax.rsqrt(jnp.sqrt(jnp.sqrt(norm2)))
    result["a"], result["y"] = a, y.astype(BF16)


class Piece:
    def __init__(self, me, nb, order, src, land, forward, xsend, xland, gath, keep, send,
                 recv, target):
        self.me, self.nb, self.order = me, nb, order
        self.src, self.land, self.forward = src, land, forward
        self.xsend, self.xland, self.gath, self.keep = xsend, xland, gath, keep
        self.send, self.recv, self.target = send, recv, target
        self.mine = lax.rem(me, 4)
        self.flow = self.run()
        self.started = []

    def partner(self, mask):
        other = self.me
        for number in range(self.nb):
            if mask >> number & 1:
                other = other + (1 - 2 * (self.me // (1 << number) % 2)) * (1 << number)
        return other

    def copy(self, src, dst, slot, mask):
        copy = pltpu.make_async_remote_copy(
            src_ref=src,
            dst_ref=dst,
            send_sem=self.send.at[slot],
            recv_sem=self.recv.at[slot],
            device_id=self.target(self.partner(mask)),
            device_id_type=MESH,
        )
        copy.start()
        self.started.append(copy)
        return copy

    def run(self):
        low = lambda mask: lax.rem(self.partner(mask), 4)
        if self.order is None:
            copies = [
                self.copy(self.src(low(mask)), self.land.at[mask - 1], mask - 1, mask)
                for mask in (1, 2, 3)
            ]
            yield
            total = self.src(self.mine)[...].astype(F32)
            for n, copy in enumerate(copies):
                copy.wait_recv()
                total += self.land[n].astype(F32)
        else:
            first, second = (1 << bit for bit in self.order)
            onward = self.copy(self.src(low(3)), self.land.at[0], 0, first)
            stay = self.copy(self.src(low(first)), self.land.at[1], 1, first)
            yield
            onward.wait_recv()
            passing = self.src(low(second))[...].astype(F32) + self.land[0].astype(F32)
            self.forward[0] = passing.astype(BF16)
            last = self.copy(self.forward.at[0], self.land.at[2], 2, second)
            yield
            stay.wait_recv()
            total = self.src(self.mine)[...].astype(F32) + self.land[1].astype(F32)
            last.wait_recv()
            total += self.land[2].astype(F32)
        for n in range(self.nb - 2):
            self.xsend[n] = total.astype(BF16)
            copy = self.copy(self.xsend.at[n], self.xland.at[n], 6 + n, 4 << n)
            if n == 0:
                yield
            copy.wait_recv()
            total = self.xsend[n].astype(F32) + self.xland[n].astype(F32)
        if self.keep is not None:
            self.keep[...] = total.astype(BF16)
            return
        self.gath(self.mine)[...] = total.astype(BF16)
        own = self.gath(self.mine)
        if self.order is None:
            copies = [self.copy(own, own, 2 + mask, mask) for mask in (1, 2, 3)]
            yield
            for copy in copies:
                copy.wait_recv()
        else:
            near = self.copy(own, own, 3, second)
            far = self.copy(own, own, 4, first)
            yield
            near.wait_recv()
            other = self.gath(low(second))
            rest = self.copy(other, other, 5, first)
            yield
            far.wait_recv()
            rest.wait_recv()

    def attend(self):
        next(self.flow, None)


def kernel(dp_count, owners, layer_ref, g_ref, out_ref, *refs):
    bufs, (acc_l, acc_r, gath_l, gath_r, columns, summed, middle, arrived, stats, whole_ref,
           e_src, e_buf, send, recv, m_send, m_recv, e_send, e_recv) = refs[:-18], refs[-18:]
    me = lax.axis_index("dp")
    own = lax.axis_index("owner")
    size_b = g_ref.shape[0]
    nb = dp_count.bit_length() - 1
    height = out_ref.shape[0]
    quarter = size_b // 4
    depth = size_b // len(GRAD_ORDERS)

    target = lambda partner: (partner, own)
    pieces = {}

    def add(name, order, src, gath, keep):
        n = len(pieces)
        land, forward, xsend, xland = bufs[4 * n:4 * n + 4]
        pieces[name] = Piece(
            me, nb, order, src, land, forward, xsend, xland, gath, keep, send.at[n], recv.at[n],
            target,
        )

    for names, orders, acc, gath in (
        ("AB", LEFT_ORDERS, acc_l, gath_l), ("CD", RIGHT_ORDERS, acc_r, gath_r)
    ):
        for p, order in enumerate(orders):
            def block(ref, p=p, rows=quarter_rows(size_b, len(orders)) + (p == 0) * EXTRA):
                return lambda q: ref.at[p, q, :rows]
            add(names[p], order, block(acc), block(gath), None)
    for n, order in enumerate(GRAD_ORDERS):
        rows = slice(n * depth, (n + 1) * depth)
        add(str(n), order, lambda q, rows=rows: columns.at[q, rows], None, summed.at[rows])
    mine_low = lax.rem(me, 4)

    barrier = pltpu.get_barrier_semaphore()
    masks = [1, 2, 3] + [4 << n for n in range(nb - 2)]
    for mask in masks:
        peer = pieces["A"].partner(mask)
        pl.semaphore_signal(barrier, inc=1, device_id=(peer, own), device_id_type=MESH)
    for j in range(1, owners):
        pl.semaphore_signal(
            barrier, inc=1, device_id=(me, lax.rem(own + j, owners)), device_id_type=MESH
        )
    g = g_ref[...]
    for q in range(4):
        columns[q] = g[:, q * quarter:(q + 1) * quarter]
    pack(
        lax.dot_general(g, g, (((1,), (1,)), ((), ())), preferred_element_type=F32),
        acc_l, size_b, len(LEFT_ORDERS),
    )
    pl.semaphore_wait(barrier, len(masks) + owners - 1)

    left, right = {}, {}
    solves = {
        "l": solver(gath_l, stats.at[0], size_b, len(LEFT_ORDERS), left),
        "r": solver(gath_r, stats.at[1], size_b, len(RIGHT_ORDERS), right),
    }
    for token in PROGRAM:
        if token == "g":
            pack(
                lax.dot_general(g, g, (((0,), (0,)), ((), ())), preferred_element_type=F32),
                acc_r, size_b, len(RIGHT_ORDERS),
            )
        elif token in solves:
            next(solves[token], None)
        elif token == "M":
            grad = summed[...]
            value = left["scale"] * (left["a"] * grad.astype(F32) + mm(left["y"], grad))
            middle[...] = value.astype(BF16).reshape(middle.shape)
            moves = []
            for mask in (1, 2, 3):
                peer = pieces["A"].partner(mask)
                move = pltpu.make_async_remote_copy(
                    src_ref=middle.at[:, lax.rem(peer, 4)],
                    dst_ref=arrived.at[mine_low],
                    send_sem=m_send.at[mask - 1],
                    recv_sem=m_recv.at[mask - 1],
                    device_id=target(peer),
                    device_id_type=MESH,
                )
                move.start()
                moves.append(move)
            arrived[mine_low] = middle[:, mine_low]
        else:
            pieces[token].attend()
    for move in moves:
        move.wait_recv()
    ours = jnp.concatenate([arrived[q].reshape(quarter, quarter) for q in range(4)], axis=1)
    whole = right["a"] * ours.astype(F32) + mm(ours, right["y"])
    whole = (right["scale"] / dp_count) * whole
    whole_ref[...] = whole.reshape(whole_ref.shape)
    energy = jnp.sum(whole * whole, keepdims=True)

    layer = layer_ref[0]
    _, lane = iotas(*e_src.shape)
    of_energy = lane == layer
    of_count = lane == layer + TILE // 2
    e_src[...] = jnp.where(of_energy, energy, jnp.where(of_count, float(quarter * size_b), 0.0))
    copies = []
    for mask in range(4):
        for j in range(owners):
            if mask + j == 0:
                continue
            n = mask * owners + j - 1
            copy = pltpu.make_async_remote_copy(
                src_ref=e_src,
                dst_ref=e_buf.at[n],
                send_sem=e_send.at[n],
                recv_sem=e_recv.at[n],
                device_id=(pieces["A"].partner(mask), lax.rem(own + j, owners)),
                device_id_type=MESH,
            )
            copy.start()
            copies.append(copy)
    for copy in moves + [copy for piece in pieces.values() for copy in piece.started]:
        copy.wait_send()
    rows = whole_ref[me // 4]
    for copy in copies:
        copy.wait()
    totals = e_src[...]
    for n in range(len(copies)):
        totals += e_buf[n]
    energies = jnp.sum(jnp.where(of_energy, totals, 0.0), keepdims=True)
    counts = jnp.sum(jnp.where(of_count, totals, 0.0), keepdims=True)
    out_ref[...] = (rows * lax.rsqrt(energies / counts + 1e-06)).astype(BF16)


def per_device(dp_count, owners, gradients, block_layer):
    size_b = gradients.shape[-1]
    nb = dp_count.bit_length() - 1
    height = size_b // dp_count
    shapes, packed = [], []
    for orders in (LEFT_ORDERS, RIGHT_ORDERS):
        rows = quarter_rows(size_b, len(orders))
        packed.append(pltpu.VMEM((len(orders), 4, rows + EXTRA, TILE), BF16))
        shapes += [(rows + (p == 0) * EXTRA, TILE) for p in range(len(orders))]
    shapes += [(size_b // len(GRAD_ORDERS), size_b // 4)] * len(GRAD_ORDERS)
    bufs = []
    for part in shapes:
        bufs += [
            pltpu.VMEM((n, *part), BF16) for n in (3, 1, nb - 2, nb - 2)
        ]
    out = pl.pallas_call(
        functools.partial(kernel, dp_count, owners),
        out_shape=jax.ShapeDtypeStruct((height, size_b), BF16),
        in_specs=[
            pl.BlockSpec(memory_space=pltpu.SMEM),
            pl.BlockSpec(memory_space=pltpu.VMEM),
        ],
        out_specs=pl.BlockSpec(memory_space=pltpu.VMEM),
        scratch_shapes=[
            *bufs,
            *packed,
            *packed,
            pltpu.VMEM((4, size_b, size_b // 4), BF16),
            pltpu.VMEM((size_b, size_b // 4), BF16),
            pltpu.VMEM((dp_count // 4, 4, height, size_b // 4), BF16),
            pltpu.VMEM((4, dp_count // 4, height, size_b // 4), BF16),
            pltpu.VMEM((2, size_b, size_b), F32),
            pltpu.VMEM((dp_count // 4, height, size_b), F32),
            pltpu.VMEM((1, TILE), F32),
            pltpu.VMEM((4 * owners - 1, 1, TILE), F32),
            pltpu.SemaphoreType.DMA((len(shapes), 4 + nb)),
            pltpu.SemaphoreType.DMA((len(shapes), 4 + nb)),
            pltpu.SemaphoreType.DMA((3,)),
            pltpu.SemaphoreType.DMA((3,)),
            pltpu.SemaphoreType.DMA((4 * owners - 1,)),
            pltpu.SemaphoreType.DMA((4 * owners - 1,)),
        ],
        compiler_params=pltpu.CompilerParams(
            collective_id=0, has_side_effects=True, vmem_limit_bytes=48 * 1024 * 1024
        ),
    )(block_layer, gradients[0, 0])
    return out[None]


def solution(mesh):
    return jax.shard_map(
        functools.partial(per_device, mesh.shape["dp"], mesh.shape["owner"]),
        mesh=mesh,
        in_specs=(P("dp", "owner", None, None), P("owner")),
        out_specs=P("owner", "dp", None),
        check_vma=False,
    )
```

time: 44.7 us -> 40.3 us (0.902)
  Pallas kernels: 42.2 us -> 37.8 us
    pallas_call x1, Pallas kernels: 42.2 us -> 37.8 us  [per_device(): pl.pallas_call(functools.partial(kernel, dp_count, owners), out_shape=jax...]
where the time goes in v2:
time: 40.3 us; the launch traced here: 40.2 us
  Pallas kernels  37.8 us (94%)
  local copies, waits for them, and re-layouts  1.67 us (4%)
  between operations  0.67 us (2%)
    pallas_call x1, Pallas kernels, per_device(): pl.pallas_call(functools.partial(kernel, dp_count, owners), out_shape=jax...  37.8 us
    unnamed x3, local copies, waits for them, and re-layouts  1.67 us

profile of v2, /device:TPU:0, one launch (start us, length us, event | category | flops | bytes accessed | tf_op | source)
XLA Modules:
  0.0 40.2 jit_solution(16879682111225110175)
XLA Ops:
  0.7 0.0 copy-start
  0.7 1.0 %copy-done = bf16[1,1,512,512]{3,2,1,0:T(8,128)(2,1)S(1)} copy-done((bf16[1,1,512,512]{3,2,1,0:T(8,128)(2,1)S(1)}, bf16[1,1,512,512]{3,2,1,0:T(8,128)(2,1)}, u32[]{:S(2)}) %copy-start) | copy-done | bytes 524312
  1.7 37.8 %shard_map.28 = bf16[64,512]{1,0:T(8,128)(2,1)S(1)} custom-call(s32[1]{0:T(128)S(6)} %copy.4.layer_ref, bf16[512,512]{1,0:T(8,128)(2,1)S(1)} %bitcast.2), custom_call_target="tpu_custom_call" | custom-call | tf_op jit(solution)/shard_map/pallas_call | solution.py:354
  39.5 0.6 %copy.5 = bf16[1,64,512]{2,1,0:T(8,128)(2,1)} copy(bf16[1,64,512]{2,1,0:T(8,128)(2,1)S(1)} %bitcast.3) | data formatting | bytes 131072
Async XLA Ops:
  0.7 1.0 %copy-start = (bf16[1,1,512,512]{3,2,1,0:T(8,128)(2,1)S(1)}, bf16[1,1,512,512]{3,2,1,0:T(8,128)(2,1)}, u32[]{:S(2)}) copy-start(bf16[1,1,512,512]{3,2,1,0:T(8,128)(2,1)} %param.2) | copy-start | bytes 1572868

commit v3 on v2

--- a/solution.py
+++ b/solution.py
@@ -12,8 +12,8 @@
 EXTRA = 16
 LEFT_ORDERS = ((0, 1), (1, 0))
 RIGHT_ORDERS = ((0, 1), (1, 0))
-GRAD_ORDERS = ((0, 1), (1, 0))
-PROGRAM = "BAgDAB1CDAB0DCA0B1CBA1DC0ABllDlC1ll0MDCrrrrr"
+GRAD_ORDERS = ((0, 1), (0, 1))
+PROGRAM = "ABgDCAB1CADB01CAB0DABC1A0DBllCllD1l0MCDrrrrr"
 BF16 = jnp.bfloat16
 F32 = jnp.float32
 MESH = pl.DeviceIdType.MESH
@@ -308,7 +308,7 @@
     of_count = lane == layer + TILE // 2
     e_src[...] = jnp.where(of_energy, energy, jnp.where(of_count, float(quarter * size_b), 0.0))
     copies = []
-    for mask in range(4):
+    for mask in (3, 2, 1, 0):
         for j in range(owners):
             if mask + j == 0:
                 continue
@@ -323,17 +323,18 @@
             )
             copy.start()
             copies.append(copy)
-    for copy in moves + [copy for piece in pieces.values() for copy in piece.started]:
-        copy.wait_send()
     rows = whole_ref[me // 4]
     for copy in copies:
-        copy.wait()
+        copy.wait_recv()
     totals = e_src[...]
     for n in range(len(copies)):
         totals += e_buf[n]
     energies = jnp.sum(jnp.where(of_energy, totals, 0.0), keepdims=True)
     counts = jnp.sum(jnp.where(of_count, totals, 0.0), keepdims=True)
     out_ref[...] = (rows * lax.rsqrt(energies / counts + 1e-06)).astype(BF16)
+    started = [copy for piece in pieces.values() for copy in piece.started]
+    for copy in started + moves + copies:
+        copy.wait_send()
 
 
 def per_device(dp_count, owners, gradients, block_layer):

time: 40.3 us -> 40 us (level)
  no operation moved by 1% of the time
where the time goes in v3:
time: 40 us; the launch traced here: 39.8 us
  Pallas kernels  37.5 us (94%)
  local copies, waits for them, and re-layouts  1.67 us (4%)
  between operations  0.67 us (2%)
    pallas_call x1, Pallas kernels, per_device(): pl.pallas_call(functools.partial(kernel, dp_count, owners), out_shape=jax...  37.5 us
    unnamed x3, local copies, waits for them, and re-layouts  1.67 us

profile of v3, /device:TPU:0, one launch (start us, length us, event | category | flops | bytes accessed | tf_op | source)
XLA Modules:
  0.0 39.8 jit_solution(5399571542001312460)
XLA Ops:
  0.7 0.0 copy-start
  0.7 1.0 %copy-done = bf16[1,1,512,512]{3,2,1,0:T(8,128)(2,1)S(1)} copy-done((bf16[1,1,512,512]{3,2,1,0:T(8,128)(2,1)S(1)}, bf16[1,1,512,512]{3,2,1,0:T(8,128)(2,1)}, u32[]{:S(2)}) %copy-start) | copy-done | bytes 524312
  1.7 37.5 %shard_map.28 = bf16[64,512]{1,0:T(8,128)(2,1)S(1)} custom-call(s32[1]{0:T(128)S(6)} %copy.4.layer_ref, bf16[512,512]{1,0:T(8,128)(2,1)S(1)} %bitcast.2), custom_call_target="tpu_custom_call" | custom-call | tf_op jit(solution)/shard_map/pallas_call | solution.py:355
  39.2 0.6 %copy.5 = bf16[1,64,512]{2,1,0:T(8,128)(2,1)} copy(bf16[1,64,512]{2,1,0:T(8,128)(2,1)S(1)} %bitcast.3) | data formatting | bytes 131072
Async XLA Ops:
  0.7 1.0 %copy-start = (bf16[1,1,512,512]{3,2,1,0:T(8,128)(2,1)S(1)}, bf16[1,1,512,512]{3,2,1,0:T(8,128)(2,1)}, u32[]{:S(2)}) copy-start(bf16[1,1,512,512]{3,2,1,0:T(8,128)(2,1)} %param.2) | copy-start | bytes 1572868
